TPU v7x, 32 devices: a whole 2x2x4 slice. The times are simulated.
32 devices in a mesh: seq: 2 (over x), mp: 4 (over y, core), dp: 4 (over z).
Axes of the slice: x: 2, y: 2, z: 4, core: 2. Of those that a mesh axis runs over, the one named last changes fastest.
Arguments:
- tokens: bfloat16 [16384, 2048], P(('dp', 'seq'), 'mp'), parts along dimension 0, may hold values from -6 to 6
- w_query: bfloat16 [2048, 2048], P(None, 'mp'), may hold values from -0.125 to 0.125
- w_key: bfloat16 [2048, 2048], P(None, 'mp'), may hold values from -0.125 to 0.125
- w_value: bfloat16 [2048, 2048], P(None, 'mp'), may hold values from -0.125 to 0.125
- w_gate: bfloat16 [2048, 2048], P(None, 'mp'), may hold values from -0.125 to 0.125
- decay_exponent: int32 [16], P('mp'), may hold values from 5 to 16
- forget: float32 [16384, 16], P(('dp', 'seq'), 'mp'), parts along dimension 0, may hold values from 0 to 0.69
- norm_gain: float32 [2048], replicated, may hold values from 0.1 to 1.9
Outputs:
- retained: bfloat16 [16384, 2048], P(('dp', 'seq', 'mp')), parts along dimension 0
There are 4 independent parts, one for each index of `dp`. A program takes and returns all parts, laid end to end along the dimension named above; an argument that names none is the same for every part. Nothing has to cross between parts.
All inputs are finite; a program needn't handle non-finite values.
Results may differ from a plain program's by a relative error of at most 0.015.
Values may be sent and summed in bfloat16 or wider, within the bound.
No kernel may reach another device: no remote copies, remote signals or barrier semaphores. Data moves between devices by JAX's collectives and lax.ppermute only.
A program may use at most 64 MiB of HBM per device.

v0:
```python
import jax
import jax.numpy as jnp
from jax import lax
from jax.sharding import PartitionSpec as P

DH = 128


def carried_in(shard, axis, join, neutral):
    place = lax.axis_index(axis)
    gathered = jax.tree.map(
        lambda a, kind: lax.all_gather(a.astype(kind), axis), shard, (jnp.bfloat16, jnp.bfloat16)
    )
    state = jax.tree.map(lambda a, e: jnp.zeros_like(a) + jnp.asarray(e, a.dtype), shard, neutral)

    def one(hop, state):
        return join(
            state,
            jax.tree.map(
                lambda a, own: lax.dynamic_index_in_dim(a, hop, 0, False).astype(own.dtype),
                gathered,
                shard,
            ),
        )

    return lax.fori_loop(0, place, one, state)


def run_blocks(queries, key_rows, values, logdecay, head_count, head_width):
    seq_rows = queries.shape[0]
    block_rows = 512
    block_count = seq_rows // block_rows

    def shaped(source):
        return source.reshape(block_count, block_rows, head_count, head_width)

    decays = logdecay.reshape(block_count, block_rows, head_count)
    position = lax.broadcasted_iota(jnp.int32, (block_rows, block_rows), 0)
    earlier = lax.broadcasted_iota(jnp.int32, (block_rows, block_rows), 1)
    causal = position >= earlier

    def advance(carried, pieces):
        kv_state, offset = carried
        query_blk, key_blk, value_blk, decay_blk = pieces
        running = jnp.cumsum(decay_blk, axis=0)
        heads_first = running.T
        log_gap = heads_first[:, :, None] - heads_first[:, None, :]
        decay_mask = jnp.where(causal[None], jnp.exp(jnp.where(causal[None], log_gap, 0.0)), 0.0)
        scores = jnp.einsum("tha,sha->hts", query_blk, key_blk, preferred_element_type=jnp.float32)
        scores = (scores * decay_mask).astype(jnp.bfloat16)
        inner = jnp.einsum("hts,shb->thb", scores, value_blk, preferred_element_type=jnp.float32)
        query_float = query_blk.astype(jnp.float32)
        earlier_part = jnp.einsum(
            "tha,hab->thb",
            query_float * jnp.exp(running)[:, :, None],
            kv_state,
            precision=lax.Precision.HIGHEST,
        )
        query_device = query_float * jnp.exp(running + offset[None, :])[:, :, None]
        key_scaled = key_blk.astype(jnp.float32) * jnp.exp(running[-1:] - running)[:, :, None]
        kv_state = jnp.exp(running[-1])[:, None, None] * kv_state + jnp.einsum(
            "sha,shb->hab",
            key_scaled,
            value_blk.astype(jnp.float32),
            precision=lax.Precision.HIGHEST,
        )
        return ((kv_state, offset + running[-1]), (inner + earlier_part, query_device))

    initial = (
        jnp.zeros((head_count, head_width, head_width), jnp.float32),
        jnp.zeros((head_count,), jnp.float32),
    )
    final, outputs = lax.scan(
        advance, initial, (shaped(queries), shaped(key_rows), shaped(values), decays)
    )
    local_part = outputs[0].reshape(seq_rows, head_count, head_width)
    query_device = outputs[1].reshape(seq_rows, head_count, head_width)
    return (local_part, query_device, final[0], final[1])


def combine_states(before, after):
    return (before[0] * after[0], after[0][:, None, None] * before[1] + after[1])


def body(tokens, w_query, w_key, w_value, w_gate, decay_exponent, forget, norm_gain):
    seq_rows = tokens.shape[0]
    local_width = w_query.shape[1]
    head_count = decay_exponent.shape[0]
    head_width = local_width // head_count
    empty = jnp.zeros((seq_rows, local_width), jnp.float32)
    summed = (empty, empty, empty, empty)
    piece = lax.all_gather(tokens, "mp", axis=1, tiled=True)
    results = []
    for weight, partial_value in zip((w_query, w_key, w_value, w_gate), summed):
        results.append(jnp.dot(piece, weight, preferred_element_type=jnp.float32))
    projected = tuple(results)
    queries = projected[0].astype(jnp.bfloat16)
    key_rows = (projected[1] * DH ** (-0.5)).astype(jnp.bfloat16)
    values = projected[2].astype(jnp.bfloat16)
    gate = projected[3].astype(jnp.bfloat16)
    rate = jnp.log1p(-jnp.exp2(-decay_exponent.astype(jnp.float32)))
    logdecay = rate[None, :] - forget
    local_part, query_device, own_state, own_total = run_blocks(
        queries, key_rows, values, logdecay, head_count, head_width
    )
    prefix = carried_in(
        (jnp.exp(own_total), own_state),
        "seq",
        combine_states,
        (jnp.ones_like(own_total), jnp.zeros_like(own_state)),
    )
    incoming = prefix[1]
    from_before = jnp.einsum(
        "tha,hab->thb", query_device, incoming, precision=lax.Precision.HIGHEST
    )
    output = (local_part + from_before).astype(jnp.bfloat16).reshape(seq_rows, local_width)
    moved_output, moved_gate = (
        lax.all_to_all(output, "mp", split_axis=0, concat_axis=1, tiled=True),
        lax.all_to_all(gate, "mp", split_axis=0, concat_axis=1, tiled=True),
    )
    output_float = moved_output.astype(jnp.float32)
    rstd = lax.rsqrt(jnp.mean(output_float * output_float, axis=1) + 1e-06)
    gated = (
        jax.nn.silu(moved_gate.astype(jnp.float32))
        * output_float
        * rstd[:, None]
        * norm_gain[None, :]
    )
    return gated.astype(jnp.bfloat16)


def solution(mesh):
    placed = (
        P(("dp", "seq"), "mp"),
        P(None, "mp"),
        P(None, "mp"),
        P(None, "mp"),
        P(None, "mp"),
        P("mp"),
        P(("dp", "seq"), "mp"),
        P(),
    )
    return jax.shard_map(
        body, mesh=mesh, in_specs=placed, out_specs=P(("dp", "seq", "mp"), None), check_vma=False
    )
```

profile of v0, /device:TPU:0, one launch (start us, length us, event | category | flops | bytes accessed | tf_op | source)
XLA Modules:
  0.0 337.5 jit_solution(5486481289894038509)
XLA Ops:
  6.5 0.7 all-gather.4.cloned.1.call-update
  7.3 1.2 dynamic-slice
  9.2 0.7 negate_log-plus-one_fusion
  9.9 0.8 broadcast_subtract_fusion
  10.7 59.2 %all-gather.4.cloned.1.call-done = bf16[2048,2048]{1,0:T(8,128)(2,1)} async-done(((bf16[2048,512]{1,0:T(8,128)(2,1)}), bf16[2048,2048]{1,0:T(8,128)(2,1)}) %all-gather.4.cloned.1.call-update) | async-done | bytes 8388624 | tf_op jit(solution)/shard_map/all_gather | solution.py:92
  69.9 9.1 %convolution_convert_fusion = bf16[2048,512]{1,0:T(8,128)(2,1)} fusion(bf16[2048,2048]{1,0:T(8,128)(2,1)} %all-gather.4.cloned.1.call-done, bf16[2048,512]{1,0:T(8,128)(2,1)S(1)} %copy-done), kind=kOutput, calls=%fused_computation.48 | convolution fusion | flops 4296015872 | bytes 12582912 | tf_op jit(solution)/shard_map/dot_general | solution.py:95
  79.0 4.0 %reshape.90 = bf16[4,512,4,128]{3,2,1,0:T(4,128)(2,1)} reshape(bf16[2048,512]{1,0:T(8,128)(2,1)} %convolution_convert_fusion) | data formatting | bytes 4194304 | tf_op jit(solution)/shard_map/reshape | solution.py:35
  83.0 8.5 %convolution_convert_fusion.1 = bf16[2048,512]{1,0:T(8,128)(2,1)S(1)} fusion(bf16[2048,2048]{1,0:T(8,128)(2,1)} %all-gather.4.cloned.1.call-done, bf16[2048,512]{1,0:T(8,128)(2,1)} %param.15), kind=kOutput, calls=%fused_computation.49 | convolution fusion | flops 4296015872 | bytes 12582912 | tf_op jit(solution)/shard_map/dot_general | solution.py:95
  91.5 2.1 reshape.89
  93.6 8.5 %multiply_convert_fusion.2 = bf16[2048,512]{1,0:T(8,128)(2,1)S(1)} fusion(bf16[2048,2048]{1,0:T(8,128)(2,1)} %all-gather.4.cloned.1.call-done, bf16[2048,512]{1,0:T(8,128)(2,1)} %param.14), kind=kOutput, calls=%fused_computation.47 | convolution fusion | flops 4297064448 | bytes 12582912 | tf_op jit(solution)/shard_map/dot_general | solution.py:95
  102.1 2.0 reshape.88
  104.1 137.0 %while.31 = (s32[]{:T(128)}, f32[4,128,128]{2,1,0:T(8,128)S(1)}, f32[4]{0:T(128)S(1)}, f32[4,512,4,128]{1,0,3,2:T(4,128)}, f32[4,512,4,128]{3,1,0,2:T(8,128)}, /...) while((s32[]{:T(128)}, f32[4,128,128]{2,1,0:T(8,128)S(1)}, ...), condition=%wide.region_3.4_spmd.clone.clone, body=%wide.region_0.3_spmd.clone.clone.sunk | while | flops 1350045696 | bytes 18760368 | solution.py:73
  104.1 1.2 reduce-window.16
  106.1 1.2 constant_dynamic-slice_fusion.5
  107.4 1.8 constant_dynamic-slice_fusion.6
  109.1 2.0 fusion.48
  111.1 1.4 fusion.49
  112.5 2.4 convolution_add_fusion.2
  114.9 1.1 copy.143
  116.0 21.0 %dynamic_update_slice.15 = f32[4,512,4,128]{1,0,3,2:T(4,128)} dynamic-update-slice(f32[4,512,4,128]{1,0,3,2:T(4,128)} %get-tuple-element.371, f32[1,512,4,128]{1,0,3,2:T(1,128)S(1)} %copy.143, s32[]{:T(128)S(6)} %copy.151, s32[]{:T(128)} %constant.52.clone.1..sunk.1, s32[]{:T(128)} %constant.52.clone.1..sunk.1, s32[]{:T(128)} %constant.52.clone.1..sunk.1) | dynamic-update-slice | bytes 2097156 | tf_op jit(solution)/shard_map/while/body/jit(dynamic_update_index_in_dim)/dynamic_update_slice | solution.py:73
  137.0 1.3 bitcast_dynamic-update-slice_fusion.2
  138.4 1.2 reduce-window.16
  140.4 1.2 constant_dynamic-slice_fusion.5
  141.6 1.8 constant_dynamic-slice_fusion.6
  143.4 2.0 fusion.48
  145.4 1.4 fusion.49
  146.7 2.4 convolution_add_fusion.2
  149.1 1.1 copy.143
  150.2 21.0 %dynamic_update_slice.15 = f32[4,512,4,128]{1,0,3,2:T(4,128)} dynamic-update-slice(f32[4,512,4,128]{1,0,3,2:T(4,128)} %get-tuple-element.371, f32[1,512,4,128]{1,0,3,2:T(1,128)S(1)} %copy.143, s32[]{:T(128)S(6)} %copy.151, s32[]{:T(128)} %constant.52.clone.1..sunk.1, s32[]{:T(128)} %constant.52.clone.1..sunk.1, s32[]{:T(128)} %constant.52.clone.1..sunk.1) | dynamic-update-slice | bytes 2097156 | tf_op jit(solution)/shard_map/while/body/jit(dynamic_update_index_in_dim)/dynamic_update_slice | solution.py:73
  171.3 1.3 bitcast_dynamic-update-slice_fusion.2
  172.6 1.2 reduce-window.16
  174.6 1.2 constant_dynamic-slice_fusion.5
  175.9 1.8 constant_dynamic-slice_fusion.6
  177.6 2.0 fusion.48
  179.6 1.4 fusion.49
  181.0 2.4 convolution_add_fusion.2
  183.4 1.1 copy.143
  184.5 21.0 %dynamic_update_slice.15 = f32[4,512,4,128]{1,0,3,2:T(4,128)} dynamic-update-slice(f32[4,512,4,128]{1,0,3,2:T(4,128)} %get-tuple-element.371, f32[1,512,4,128]{1,0,3,2:T(1,128)S(1)} %copy.143, s32[]{:T(128)S(6)} %copy.151, s32[]{:T(128)} %constant.52.clone.1..sunk.1, s32[]{:T(128)} %constant.52.clone.1..sunk.1, s32[]{:T(128)} %constant.52.clone.1..sunk.1) | dynamic-update-slice | bytes 2097156 | tf_op jit(solution)/shard_map/while/body/jit(dynamic_update_index_in_dim)/dynamic_update_slice | solution.py:73
  205.5 1.3 bitcast_dynamic-update-slice_fusion.2
  206.9 1.2 reduce-window.16
  208.9 1.2 constant_dynamic-slice_fusion.5
  210.1 1.8 constant_dynamic-slice_fusion.6
  211.9 2.0 fusion.48
  213.9 1.4 fusion.49
  215.2 2.4 convolution_add_fusion.2
  217.6 1.1 copy.143
  218.7 21.0 %dynamic_update_slice.15 = f32[4,512,4,128]{1,0,3,2:T(4,128)} dynamic-update-slice(f32[4,512,4,128]{1,0,3,2:T(4,128)} %get-tuple-element.371, f32[1,512,4,128]{1,0,3,2:T(1,128)S(1)} %copy.143, s32[]{:T(128)S(6)} %copy.151, s32[]{:T(128)} %constant.52.clone.1..sunk.1, s32[]{:T(128)} %constant.52.clone.1..sunk.1, s32[]{:T(128)} %constant.52.clone.1..sunk.1) | dynamic-update-slice | bytes 2097156 | tf_op jit(solution)/shard_map/while/body/jit(dynamic_update_index_in_dim)/dynamic_update_slice | solution.py:73
  239.8 1.3 bitcast_dynamic-update-slice_fusion.2
  241.4 9.8 %convolution_convert_fusion.2 = bf16[2048,512]{1,0:T(8,128)(2,1)} fusion(bf16[2048,2048]{1,0:T(8,128)(2,1)} %all-gather.4.cloned.1.call-done, bf16[2048,512]{1,0:T(8,128)(2,1)} %param.16), kind=kOutput, calls=%fused_computation.50 | convolution fusion | flops 4296015872 | bytes 12582912 | tf_op jit(solution)/shard_map/dot_general | solution.py:95
  251.2 4.4 %all-to-all-start = ((bf16[4,512,512]{2,1,0:T(8,128)(2,1)}), bf16[4,512,512]{2,1,0:T(8,128)(2,1)}, u32[]{:S(2)}, u32[]{:S(2)}) async-start(bf16[4,512,512]{2,1,0:T(8,128)(2,1)} %bitcast.2), calls=%async_computation | async-start | bytes 4194304 | tf_op jit(solution)/shard_map/all_to_all | solution.py:119
  255.7 4.9 %all-reduce = bf16[8]{0:T(256)(128)(2,1)S(1)} all-reduce(bf16[8]{0:T(256)(128)(2,1)S(1)} %dynamic-update-slice), channel_id=2, replica_groups=mesh['seq'=2,'mp'=4,'dp'=4] {'seq'}, use_global_device_ids=true, to_apply=%add | all-reduce | flops 8 | bytes 32
  260.7 5.7 %all-gather.1 = bf16[8,128,128]{2,1,0:T(8,128)(2,1)S(1)} all-gather(bf16[4,128,128]{2,1,0:T(8,128)(2,1)S(1)} %convert_element_type.89), channel_id=3, replica_groups=mesh['seq'=2,'mp'=4,'dp'=4] {'seq'}, dimensions={0}, use_global_device_ids=true | all-gather | bytes 393216 | tf_op jit(solution)/shard_map/all_gather | solution.py:12
  266.4 6.1 %reshape.91 = f32[2048,4,128]{0,2,1:T(8,128)} reshape(f32[4,512,4,128]{1,0,3,2:T(4,128)} %get-tuple-element.107) | data formatting | bytes 8388608 | tf_op jit(solution)/shard_map/reshape | solution.py:76
  272.5 8.8 %fusion.24 = bf16[2048,4,128]{0,2,1:T(8,128)(2,1)} fusion(f32[2048,4,128]{0,2,1:T(8,128)} %reshape.91, f32[4,128,128]{2,1,0:T(8,128)S(1)} %get-tuple-element.110, f32[2048,4,128]{2,0,1:T(8,128)} %bitcast.128), kind=kOutput, calls=%fused_computation.43 | convolution fusion | flops 1612709888 | bytes 10747904 | tf_op jit(solution)/shard_map/tha,hab->thb/dot_general | solution.py:113
  281.4 3.3 all_to_all.22
  284.7 1.7 copy.79
  286.4 3.6 %all-to-all-start.1 = ((bf16[4,512,512]{1,2,0:T(8,128)(2,1)}), bf16[4,512,512]{1,2,0:T(8,128)(2,1)S(1)}, u32[]{:S(2)}, u32[]{:S(2)}) async-start(bf16[4,512,512]{1,2,0:T(8,128)(2,1)} %copy.79), calls=%async_computation.1 | async-start | bytes 4194304 | tf_op jit(solution)/shard_map/all_to_all | solution.py:118
  290.0 2.2 convert_bitcast_fusion
  292.2 2.6 copy.94
  294.8 20.9 %all-to-all-done.1 = bf16[4,512,512]{1,2,0:T(8,128)(2,1)S(1)} async-done(((bf16[4,512,512]{1,2,0:T(8,128)(2,1)}), bf16[4,512,512]{1,2,0:T(8,128)(2,1)S(1)}, u32[]{:S(2)}, u32[]{:S(2)}) %all-to-all-start.1) | async-done | bytes 2097184 | tf_op jit(solution)/shard_map/all_to_all | solution.py:118
  315.7 0.5 multiply_reduce_fusion
  316.2 2.6 convert_element_type.105
  318.8 5.4 %copy.80 = f32[512,2048]{1,0:T(8,128)} copy(f32[512,2048]{0,1:T(8,128)} %bitcast.127) | data formatting | bytes 8388608 | tf_op jit(solution)/shard_map/convert_element_type | solution.py:121
  324.2 6.4 %multiply_convert_fusion.1 = bf16[512,2048]{1,0:T(8,128)(2,1)} fusion(f32[512,2048]{1,0:T(8,128)} %copy.80, f32[512,2048]{1,0:T(8,128)} %bitcast.126, f32[2048]{0:T(1024)S(1)} %copy-done.3, f32[512]{0:T(512)S(1)} %add_rsqrt_fusion), kind=kLoop, calls=%fused_computation.45 | loop fusion | flops 8388608 | bytes 10496000 | tf_op jit(solution)/shard_map/convert_element_type | solution.py:129
  (68 shorter events, 3.6 us)
Async XLA Ops:
  6.5 63.4 %copy-start = (bf16[2048,512]{1,0:T(8,128)(2,1)S(1)}, bf16[2048,512]{1,0:T(8,128)(2,1)}, u32[]{:S(2)}) copy-start(bf16[2048,512]{1,0:T(8,128)(2,1)} %param.13) | copy-start | bytes 6291460
  6.5 63.4 %all-gather.4.cloned.1.call-start = ((), (), s32[]{:S(2)}) async-start(), calls=%async_computation.2 | async-start | bytes 10485760 | tf_op jit(solution)/shard_map/all_gather | solution.py:92
  107.4 1.8 copy-start.2
  141.6 1.8 copy-start.2
  175.9 1.8 copy-start.2
  210.1 1.8 copy-start.2
  251.2 35.2 %all-to-all-start = ((bf16[4,512,512]{2,1,0:T(8,128)(2,1)}), bf16[4,512,512]{2,1,0:T(8,128)(2,1)}, u32[]{:S(2)}, u32[]{:S(2)}) async-start(bf16[4,512,512]{2,1,0:T(8,128)(2,1)} %bitcast.2), calls=%async_computation | async-start | bytes 4194304 | tf_op jit(solution)/shard_map/all_to_all | solution.py:119
  286.4 29.3 %all-to-all-start.1 = ((bf16[4,512,512]{1,2,0:T(8,128)(2,1)}), bf16[4,512,512]{1,2,0:T(8,128)(2,1)S(1)}, u32[]{:S(2)}, u32[]{:S(2)}) async-start(bf16[4,512,512]{1,2,0:T(8,128)(2,1)} %copy.79), calls=%async_computation.1 | async-start | bytes 4194304 | tf_op jit(solution)/shard_map/all_to_all | solution.py:118
  318.8 5.4 %copy-start.3 = (f32[2048]{0:T(1024)S(1)}, f32[2048]{0:T(1024)}, u32[]{:S(2)}) copy-start(f32[2048]{0:T(1024)} %param.19) | copy-start | bytes 24580
  324.2 6.4 %copy-start.1 = (bf16[2048,512]{1,0:T(8,128)(2,1)S(1)}, bf16[2048,512]{1,0:T(8,128)(2,1)}, u32[]{:S(2)}) copy-start(bf16[2048,512]{1,0:T(8,128)(2,1)} %param.13) | copy-start | bytes 6291460
Sparse Core Ops, SparseCore 0:
  8.9 60.9 all-gather.3
where the time goes:
time: 341 us; the launch traced here: 337 us
  local copies, waits for them, and re-layouts  131 us (38%)
  waiting for transfers between devices  80.8 us (24%)
  matrix products  67.6 us (20%)
  other arithmetic  25.1 us (7%)
  between operations  14.2 us (4%)
  blocking collectives  10.7 us (3%)
  starting transfers between devices  8.06 us (2%)
    dynamic_update_slice x8, local copies, waits for them, and re-layouts, run_blocks(): lax.scan(advance, initial, (shaped(queries), shaped(key_rows), shaped(val...  88.5 us
    all_gather x1, waiting for transfers between devices, body(): piece = lax.all_gather(tokens, 'mp', axis=1, tiled=True)  59.2 us
    dot_general x4, matrix products, body(): results.append(jnp.dot(piece, weight, preferred_element_type=jnp.float32))  35.9 us
    all_to_all x1, waiting for transfers between devices, body(): lax.all_to_all(output, 'mp', split_axis=0, concat_axis=1, tiled=True)  20.9 us
    dynamic_slice x8, local copies, waits for them, and re-layouts, run_blocks(): lax.scan(advance, initial, (shaped(queries), shaped(key_rows), shaped(val...  11.9 us
    dot_general x4, matrix products, advance(): jnp.einsum('sha,shb->hab', key_scaled, value_blk.astype(jnp.float32), pre...  9.56 us
    dot_general x1, matrix products, body(): jnp.einsum('tha,hab->thb', query_device, incoming, precision=lax.Precisio...  8.83 us
    reshape x3, local copies, waits for them, and re-layouts, shaped(): return source.reshape(block_count, block_rows, head_count, head_width)  8.09 us
  transfers between devices with their start and end apart: 3, of which 2 were waited for; matrix products, arithmetic and copies ran while one was open for 7% of the time, Pallas kernels for 0%

commit v1 on v0

--- a/solution.py
+++ b/solution.py
@@ -89,7 +89,7 @@
     head_width = local_width // head_count
     empty = jnp.zeros((seq_rows, local_width), jnp.float32)
     summed = (empty, empty, empty, empty)
-    piece = lax.all_gather(tokens, "mp", axis=1, tiled=True)
+    piece = jnp.concatenate(lax.all_gather(tokens, "mp"), axis=1)
     results = []
     for weight, partial_value in zip((w_query, w_key, w_value, w_gate), summed):
         results.append(jnp.dot(piece, weight, preferred_element_type=jnp.float32))

time: 341 us -> 353 us (1.035)
  local copies, waits for them, and re-layouts: 131 us -> 142 us
    reshape x4 -> x5, local copies, waits for them, and re-layouts: 0.07 us -> 11.5 us  [the longest x1 11.4 us: body(): piece = jnp.concatenate(lax.all_gather(tokens, 'mp'), axis=1)]
where the time goes in v1:
time: 353 us; the launch traced here: 349 us
  local copies, waits for them, and re-layouts  142 us (40%)
  waiting for transfers between devices  80.8 us (23%)
  matrix products  68 us (19%)
  other arithmetic  25.1 us (7%)
  between operations  14.2 us (4%)
  blocking collectives  10.7 us (3%)
  starting transfers between devices  8.07 us (2%)
    dynamic_update_slice x8, local copies, waits for them, and re-layouts, run_blocks(): lax.scan(advance, initial, (shaped(queries), shaped(key_rows), shaped(val...  88.4 us
    all_gather x1, waiting for transfers between devices, body(): piece = jnp.concatenate(lax.all_gather(tokens, 'mp'), axis=1)  59.2 us
    dot_general x4, matrix products, body(): results.append(jnp.dot(piece, weight, preferred_element_type=jnp.float32))  36.3 us
    all_to_all x1, waiting for transfers between devices, body(): lax.all_to_all(output, 'mp', split_axis=0, concat_axis=1, tiled=True)  20.9 us
    dynamic_slice x8, local copies, waits for them, and re-layouts, run_blocks(): lax.scan(advance, initial, (shaped(queries), shaped(key_rows), shaped(val...  11.9 us
    reshape x1, local copies, waits for them, and re-layouts, body(): piece = jnp.concatenate(lax.all_gather(tokens, 'mp'), axis=1)  11.4 us
    dot_general x4, matrix products, advance(): jnp.einsum('sha,shb->hab', key_scaled, value_blk.astype(jnp.float32), pre...  9.56 us
    dot_general x1, matrix products, body(): jnp.einsum('tha,hab->thb', query_device, incoming, precision=lax.Precisio...  8.83 us
  transfers between devices with their start and end apart: 3, of which 2 were waited for; matrix products, arithmetic and copies ran while one was open for 7% of the time, Pallas kernels for 0%

profile of v1, /device:TPU:0, one launch (start us, length us, event | category | flops | bytes accessed | tf_op | source)
XLA Modules:
  0.0 349.3 jit_solution(14921024207149176118)
XLA Ops:
  6.5 0.7 all-gather.5.cloned.1.call-update
  7.3 1.2 dynamic-slice
  9.2 0.7 negate_log-plus-one_fusion
  9.9 0.8 broadcast_subtract_fusion
  10.7 59.2 %all-gather.5.cloned.1.call-done = bf16[8192,512]{1,0:T(8,128)(2,1)} async-done(((bf16[2048,512]{1,0:T(8,128)(2,1)}), bf16[8192,512]{1,0:T(8,128)(2,1)}) %all-gather.5.cloned.1.call-update) | async-done | bytes 8388624 | tf_op jit(solution)/shard_map/all_gather | solution.py:92
  69.9 11.4 %copy.90 = bf16[2048,4,512]{0,2,1:T(8,128)(2,1)} copy(bf16[2048,4,512]{2,0,1:T(8,128)(2,1)} %bitcast.132) | data formatting | bytes 16777216 | tf_op jit(solution)/shard_map/reshape | solution.py:92
  81.3 9.4 %convolution_convert_fusion = bf16[2048,512]{1,0:T(8,128)(2,1)} fusion(bf16[2048,2048]{0,1:T(8,128)(2,1)} %bitcast.133, bf16[2048,512]{1,0:T(8,128)(2,1)S(1)} %copy-done), kind=kOutput, calls=%fused_computation.48 | convolution fusion | flops 4296015872 | bytes 12582912 | tf_op jit(solution)/shard_map/dot_general | solution.py:95
  90.7 4.0 %reshape.98 = bf16[4,512,4,128]{3,2,1,0:T(4,128)(2,1)} reshape(bf16[2048,512]{1,0:T(8,128)(2,1)} %convolution_convert_fusion) | data formatting | bytes 4194304 | tf_op jit(solution)/shard_map/reshape | solution.py:35
  94.7 8.5 %convolution_convert_fusion.1 = bf16[2048,512]{1,0:T(8,128)(2,1)S(1)} fusion(bf16[2048,2048]{0,1:T(8,128)(2,1)} %bitcast.134, bf16[2048,512]{1,0:T(8,128)(2,1)} %param.15), kind=kOutput, calls=%fused_computation.49 | convolution fusion | flops 4296015872 | bytes 12582912 | tf_op jit(solution)/shard_map/dot_general | solution.py:95
  103.2 2.1 reshape.97
  105.3 8.7 %multiply_convert_fusion.2 = bf16[2048,512]{1,0:T(8,128)(2,1)S(1)} fusion(bf16[2048,2048]{0,1:T(8,128)(2,1)} %bitcast.135, bf16[2048,512]{1,0:T(8,128)(2,1)} %param.14), kind=kOutput, calls=%fused_computation.47 | convolution fusion | flops 4297064448 | bytes 12582912 | tf_op jit(solution)/shard_map/dot_general | solution.py:95
  114.0 9.7 %convolution_convert_fusion.2 = bf16[2048,512]{1,0:T(8,128)(2,1)} fusion(bf16[2048,2048]{0,1:T(8,128)(2,1)} %bitcast.136, bf16[2048,512]{1,0:T(8,128)(2,1)S(1)} %copy-done.4), kind=kOutput, calls=%fused_computation.50 | convolution fusion | flops 4296015872 | bytes 12582912 | tf_op jit(solution)/shard_map/dot_general | solution.py:95
  123.7 2.0 reshape.96
  125.7 136.8 %while.31 = (s32[]{:T(128)}, f32[4,128,128]{2,1,0:T(8,128)S(1)}, f32[4]{0:T(128)S(1)}, f32[4,512,4,128]{1,0,3,2:T(4,128)}, f32[4,512,4,128]{3,1,0,2:T(8,128)}, /...) while((s32[]{:T(128)}, f32[4,128,128]{2,1,0:T(8,128)S(1)}, ...), condition=%wide.region_3.4_spmd.clone.clone, body=%wide.region_0.3_spmd.clone.clone.sunk | while | flops 1350045696 | bytes 18760368 | solution.py:73
  125.7 1.2 reduce-window.16
  127.7 1.2 constant_dynamic-slice_fusion.5
  129.0 1.8 constant_dynamic-slice_fusion.6
  130.8 2.0 fusion.48
  132.7 1.4 fusion.49
  134.1 2.4 convolution_add_fusion.2
  136.5 1.1 copy.163
  137.6 21.0 %dynamic_update_slice.15 = f32[4,512,4,128]{1,0,3,2:T(4,128)} dynamic-update-slice(f32[4,512,4,128]{1,0,3,2:T(4,128)} %get-tuple-element.380, f32[1,512,4,128]{1,0,3,2:T(1,128)S(1)} %copy.163, s32[]{:T(128)S(6)} %copy.171, s32[]{:T(128)} %constant.52.clone.1..sunk.1, s32[]{:T(128)} %constant.52.clone.1..sunk.1, s32[]{:T(128)} %constant.52.clone.1..sunk.1) | dynamic-update-slice | bytes 2097156 | tf_op jit(solution)/shard_map/while/body/jit(dynamic_update_index_in_dim)/dynamic_update_slice | solution.py:73
  158.6 1.4 bitcast_dynamic-update-slice_fusion.2
  160.0 1.2 reduce-window.16
  162.0 1.2 constant_dynamic-slice_fusion.5
  163.2 1.8 constant_dynamic-slice_fusion.6
  165.0 2.0 fusion.48
  167.0 1.4 fusion.49
  168.3 2.4 convolution_add_fusion.2
  170.7 1.1 copy.163
  171.8 21.0 %dynamic_update_slice.15 = f32[4,512,4,128]{1,0,3,2:T(4,128)} dynamic-update-slice(f32[4,512,4,128]{1,0,3,2:T(4,128)} %get-tuple-element.380, f32[1,512,4,128]{1,0,3,2:T(1,128)S(1)} %copy.163, s32[]{:T(128)S(6)} %copy.171, s32[]{:T(128)} %constant.52.clone.1..sunk.1, s32[]{:T(128)} %constant.52.clone.1..sunk.1, s32[]{:T(128)} %constant.52.clone.1..sunk.1) | dynamic-update-slice | bytes 2097156 | tf_op jit(solution)/shard_map/while/body/jit(dynamic_update_index_in_dim)/dynamic_update_slice | solution.py:73
  192.8 1.3 bitcast_dynamic-update-slice_fusion.2
  194.2 1.2 reduce-window.16
  196.2 1.2 constant_dynamic-slice_fusion.5
  197.5 1.8 constant_dynamic-slice_fusion.6
  199.2 2.0 fusion.48
  201.2 1.4 fusion.49
  202.6 2.4 convolution_add_fusion.2
  205.0 1.1 copy.163
  206.1 21.0 %dynamic_update_slice.15 = f32[4,512,4,128]{1,0,3,2:T(4,128)} dynamic-update-slice(f32[4,512,4,128]{1,0,3,2:T(4,128)} %get-tuple-element.380, f32[1,512,4,128]{1,0,3,2:T(1,128)S(1)} %copy.163, s32[]{:T(128)S(6)} %copy.171, s32[]{:T(128)} %constant.52.clone.1..sunk.1, s32[]{:T(128)} %constant.52.clone.1..sunk.1, s32[]{:T(128)} %constant.52.clone.1..sunk.1) | dynamic-update-slice | bytes 2097156 | tf_op jit(solution)/shard_map/while/body/jit(dynamic_update_index_in_dim)/dynamic_update_slice | solution.py:73
  227.1 1.3 bitcast_dynamic-update-slice_fusion.2
  228.4 1.2 reduce-window.16
  230.4 1.2 constant_dynamic-slice_fusion.5
  231.6 1.8 constant_dynamic-slice_fusion.6
  233.4 2.0 fusion.48
  235.4 1.4 fusion.49
  236.8 2.4 convolution_add_fusion.2
  239.1 1.1 copy.163
  240.2 21.0 %dynamic_update_slice.15 = f32[4,512,4,128]{1,0,3,2:T(4,128)} dynamic-update-slice(f32[4,512,4,128]{1,0,3,2:T(4,128)} %get-tuple-element.380, f32[1,512,4,128]{1,0,3,2:T(1,128)S(1)} %copy.163, s32[]{:T(128)S(6)} %copy.171, s32[]{:T(128)} %constant.52.clone.1..sunk.1, s32[]{:T(128)} %constant.52.clone.1..sunk.1, s32[]{:T(128)} %constant.52.clone.1..sunk.1) | dynamic-update-slice | bytes 2097156 | tf_op jit(solution)/shard_map/while/body/jit(dynamic_update_index_in_dim)/dynamic_update_slice | solution.py:73
  261.2 1.3 bitcast_dynamic-update-slice_fusion.2
  262.8 4.5 %all-to-all-start = ((bf16[4,512,512]{2,1,0:T(8,128)(2,1)}), bf16[4,512,512]{2,1,0:T(8,128)(2,1)}, u32[]{:S(2)}, u32[]{:S(2)}) async-start(bf16[4,512,512]{2,1,0:T(8,128)(2,1)} %bitcast.139), calls=%async_computation | async-start | bytes 4194304 | tf_op jit(solution)/shard_map/all_to_all | solution.py:119
  267.3 4.9 %all-reduce = bf16[8]{0:T(256)(128)(2,1)S(1)} all-reduce(bf16[8]{0:T(256)(128)(2,1)S(1)} %dynamic-update-slice), channel_id=3, replica_groups=mesh['seq'=2,'mp'=4,'dp'=4] {'seq'}, use_global_device_ids=true, to_apply=%add | all-reduce | flops 8 | bytes 32
  272.3 5.7 %all-gather.2 = bf16[8,128,128]{2,1,0:T(8,128)(2,1)S(1)} all-gather(bf16[4,128,128]{2,1,0:T(8,128)(2,1)S(1)} %convert_element_type.89), channel_id=4, replica_groups=mesh['seq'=2,'mp'=4,'dp'=4] {'seq'}, dimensions={0}, use_global_device_ids=true | all-gather | bytes 393216 | tf_op jit(solution)/shard_map/all_gather | solution.py:12
  278.1 6.1 %reshape.99 = f32[2048,4,128]{0,2,1:T(8,128)} reshape(f32[4,512,4,128]{1,0,3,2:T(4,128)} %get-tuple-element.107) | data formatting | bytes 8388608 | tf_op jit(solution)/shard_map/reshape | solution.py:76
  284.4 8.8 %fusion.24 = bf16[2048,4,128]{0,2,1:T(8,128)(2,1)} fusion(f32[2048,4,128]{0,2,1:T(8,128)} %reshape.99, f32[4,128,128]{2,1,0:T(8,128)S(1)} %get-tuple-element.110, f32[2048,4,128]{2,0,1:T(8,128)} %bitcast.137), kind=kOutput, calls=%fused_computation.43 | convolution fusion | flops 1612709888 | bytes 10747904 | tf_op jit(solution)/shard_map/tha,hab->thb/dot_general | solution.py:113
  293.2 3.3 all_to_all.22
  296.5 1.7 copy.99
  298.3 3.6 %all-to-all-start.1 = ((bf16[4,512,512]{1,2,0:T(8,128)(2,1)}), bf16[4,512,512]{1,2,0:T(8,128)(2,1)S(1)}, u32[]{:S(2)}, u32[]{:S(2)}) async-start(bf16[4,512,512]{1,2,0:T(8,128)(2,1)} %copy.99), calls=%async_computation.1 | async-start | bytes 4194304 | tf_op jit(solution)/shard_map/all_to_all | solution.py:118
  301.9 2.2 convert_bitcast_fusion
  304.1 2.6 copy.114
  306.6 20.9 %all-to-all-done.1 = bf16[4,512,512]{1,2,0:T(8,128)(2,1)S(1)} async-done(((bf16[4,512,512]{1,2,0:T(8,128)(2,1)}), bf16[4,512,512]{1,2,0:T(8,128)(2,1)S(1)}, u32[]{:S(2)}, u32[]{:S(2)}) %all-to-all-start.1) | async-done | bytes 2097184 | tf_op jit(solution)/shard_map/all_to_all | solution.py:118
  328.0 2.6 convert_element_type.105
  330.6 5.4 %copy.100 = f32[512,2048]{1,0:T(8,128)} copy(f32[512,2048]{0,1:T(8,128)} %bitcast.131) | data formatting | bytes 8388608 | tf_op jit(solution)/shard_map/convert_element_type | solution.py:121
  336.0 6.4 %multiply_convert_fusion.1 = bf16[512,2048]{1,0:T(8,128)(2,1)} fusion(f32[512,2048]{1,0:T(8,128)} %copy.100, f32[512,2048]{1,0:T(8,128)} %bitcast.130, f32[2048]{0:T(1024)S(1)} %copy-done.3, f32[512]{0:T(512)S(1)} %add_rsqrt_fusion), kind=kLoop, calls=%fused_computation.45 | loop fusion | flops 8388608 | bytes 10496000 | tf_op jit(solution)/shard_map/convert_element_type | solution.py:129
  (71 shorter events, 4.4 us)
Async XLA Ops:
  6.5 74.8 %copy-start = (bf16[2048,512]{1,0:T(8,128)(2,1)S(1)}, bf16[2048,512]{1,0:T(8,128)(2,1)}, u32[]{:S(2)}) copy-start(bf16[2048,512]{1,0:T(8,128)(2,1)} %param.13) | copy-start | bytes 6291460
  6.5 63.4 %all-gather.5.cloned.1.call-start = ((), (), s32[]{:S(2)}) async-start(), calls=%async_computation.2 | async-start | bytes 10485760 | tf_op jit(solution)/shard_map/all_gather | solution.py:92
  105.3 8.7 %copy-start.4 = (bf16[2048,512]{1,0:T(8,128)(2,1)S(1)}, bf16[2048,512]{1,0:T(8,128)(2,1)}, u32[]{:S(2)}) copy-start(bf16[2048,512]{1,0:T(8,128)(2,1)} %param.16) | copy-start | bytes 6291460
  129.0 1.8 copy-start.2
  163.2 1.8 copy-start.2
  197.4 1.8 copy-start.2
  231.6 1.8 copy-start.2
  262.8 35.5 %all-to-all-start = ((bf16[4,512,512]{2,1,0:T(8,128)(2,1)}), bf16[4,512,512]{2,1,0:T(8,128)(2,1)}, u32[]{:S(2)}, u32[]{:S(2)}) async-start(bf16[4,512,512]{2,1,0:T(8,128)(2,1)} %bitcast.139), calls=%async_computation | async-start | bytes 4194304 | tf_op jit(solution)/shard_map/all_to_all | solution.py:119
  298.3 29.3 %all-to-all-start.1 = ((bf16[4,512,512]{1,2,0:T(8,128)(2,1)}), bf16[4,512,512]{1,2,0:T(8,128)(2,1)S(1)}, u32[]{:S(2)}, u32[]{:S(2)}) async-start(bf16[4,512,512]{1,2,0:T(8,128)(2,1)} %copy.99), calls=%async_computation.1 | async-start | bytes 4194304 | tf_op jit(solution)/shard_map/all_to_all | solution.py:118
  330.6 5.4 %copy-start.3 = (f32[2048]{0:T(1024)S(1)}, f32[2048]{0:T(1024)}, u32[]{:S(2)}) copy-start(f32[2048]{0:T(1024)} %param.19) | copy-start | bytes 24580
  336.0 6.4 %copy-start.1 = (bf16[2048,512]{1,0:T(8,128)(2,1)S(1)}, bf16[2048,512]{1,0:T(8,128)(2,1)}, u32[]{:S(2)}) copy-start(bf16[2048,512]{1,0:T(8,128)(2,1)} %param.13) | copy-start | bytes 6291460
Sparse Core Ops, SparseCore 0:
  8.9 60.9 all-gather.4
